TPU v7x, 32 devices: a whole 2x2x4 slice. The times are simulated.
32 devices in a mesh: dp: 8 (over z, x), tensor: 4 (over y, core).
Axes of the slice: x: 2, y: 2, z: 4, core: 2. Of those that a mesh axis runs over, the one named last changes fastest.
Arguments:
- latents: bfloat16 [32, 512, 1024], P(('dp', 'tensor')), may hold values from -6 to 6
- cotangent: bfloat16 [32, 512, 1024], P(('dp', 'tensor')), may hold values from -6 to 6
- counts: int32 [16], replicated, may hold values from 1 to 3, as said below
- assign: int32 [16], replicated, may hold values from 0 to 7, as said below
- pre_gain: float32 [1024], replicated, may hold values from 0.1 to 1.9
- pre_shift: float32 [1024], replicated, may hold values from -1.75 to 1.75
- w_query: bfloat16 [1024, 1024], P(None, 'tensor'), may hold values from -0.375 to 0.375
- b_query: float32 [1024], P('tensor'), may hold values from -3 to 3
- w_key: bfloat16 [1024, 1024], P(None, 'tensor'), may hold values from -0.1875 to 0.1875
- w_value: bfloat16 [1024, 1024], P(None, 'tensor'), may hold values from -0.1875 to 0.1875
- b_value: float32 [1024], P('tensor'), may hold values from -1.75 to 1.75
- w_out: bfloat16 [1024, 1024], P('tensor'), may hold values from -0.75 to 0.75
- b_out: float32 [1024], replicated, may hold values from -1.75 to 1.75
- mid_gain: float32 [1024], replicated, may hold values from 0.1 to 1.9
- mid_shift: float32 [1024], replicated, may hold values from -1.75 to 1.75
- w_up: bfloat16 [1024, 1024], P(None, 'tensor'), may hold values from -0.1875 to 0.1875
- b_up: float32 [1024], P('tensor'), may hold values from -1.75 to 1.75
- w_down: bfloat16 [1024, 1024], P('tensor'), may hold values from -0.25 to 0.25
- b_down: float32 [1024], replicated, may hold values from -1.75 to 1.75
Outputs:
- latents_out: bfloat16 [32, 512, 1024], P(('dp', 'tensor'))
- latents_grad: float32 [32, 512, 1024], P(('dp', 'tensor'))
- pregain_grad: float32 [1024], replicated
- preshift_grad: float32 [1024], replicated
- wquery_grad: float32 [1024, 1024], P(None, 'tensor')
- bquery_grad: float32 [1024], P('tensor')
- wkey_grad: float32 [1024, 1024], P(None, 'tensor')
- wvalue_grad: float32 [1024, 1024], P(None, 'tensor')
- bvalue_grad: float32 [1024], P('tensor')
- wout_grad: float32 [1024, 1024], P('tensor')
- bout_grad: float32 [1024], replicated
- midgain_grad: float32 [1024], replicated
- midshift_grad: float32 [1024], replicated
- wup_grad: float32 [1024, 1024], P(None, 'tensor')
- bup_grad: float32 [1024], P('tensor')
- wdown_grad: float32 [1024, 1024], P('tensor')
- bdown_grad: float32 [1024], replicated
Inputs may be any that keep to these rules, and one draw needn't show every extreme that they name: The counts of the 2 images of one data index add up to at most 4, and to exactly 4 on at least one data index. `assign`: each data index holds exactly 2 images.
All inputs are finite; a program needn't handle non-finite values.
Results may differ from a plain program's by a relative error of at most 0.017.
Values may be sent and summed in bfloat16 or wider, within the bound.
A program may use at most 128 MiB of HBM per device.

v0:
```python
from functools import partial
import math
import jax
import jax.numpy as jnp
from jax import lax
from jax.sharding import PartitionSpec as P

HEAD = 128
epsilon = 1e-05


def normalize(inputs, norm_gain, norm_shift):
    center = jnp.mean(inputs, axis=-1, keepdims=True)
    centered = inputs - center
    inverse = lax.rsqrt(jnp.mean(centered * centered, axis=-1, keepdims=True) + epsilon)
    scaled = centered * inverse
    return (scaled * norm_gain + norm_shift, scaled, inverse)


def norm_backward(upstream, scaled, inverse, norm_gain):
    weighted = upstream * norm_gain
    first_mean = jnp.mean(weighted, axis=-1, keepdims=True)
    second_mean = jnp.mean(weighted * scaled, axis=-1, keepdims=True)
    return inverse * (weighted - first_mean - scaled * second_mean)


def shards(
    latents,
    cotangent,
    counts,
    assign,
    pre_gain,
    pre_shift,
    w_query,
    b_query,
    w_key,
    w_value,
    b_value,
    w_out,
    b_out,
    mid_gain,
    mid_shift,
    w_up,
    b_up,
    w_down,
    b_down,
):
    f32, bf16 = (jnp.float32, jnp.bfloat16)
    crops, length, width = latents.shape
    tensor = lax.axis_size("tensor")
    heads = width // HEAD
    group_total = jnp.sum(jnp.where(assign == lax.axis_index("dp"), counts, 0))
    slot_ids = lax.axis_index("tensor") * crops + jnp.arange(crops, dtype=jnp.int32)
    live = jnp.repeat((slot_ids < group_total).astype(f32), length)[:, None]
    scaling = 1.0 / math.sqrt(HEAD)

    def dot(left, right, dims):
        return lax.dot_general(left, right, (dims, ((), ())), preferred_element_type=f32)

    columns = jnp.concatenate([w_query.T, w_key.T, w_value.T, w_out, w_up.T, w_down], axis=0)
    per = w_query.shape[1]
    gathered = lax.all_gather(columns, "tensor", axis=0, tiled=False).reshape(tensor, 6, per, width)
    wq, wk, wv, wo, wu, wd = [gathered[:, i].reshape(tensor * per, width) for i in range(6)]
    bias = lax.all_gather(jnp.stack([b_query, b_value, b_up]), "tensor", axis=1, tiled=True)
    rows = latents.astype(f32).reshape(crops * length, width)
    normed, scaled, inverse = normalize(rows, pre_gain, pre_shift)
    normed = normed.astype(bf16)
    q = (dot(normed, wq, ((1,), (1,))) + bias[0]).astype(bf16)
    k = dot(normed, wk, ((1,), (1,))).astype(bf16)
    v = (dot(normed, wv, ((1,), (1,))) + bias[1]).astype(bf16)
    split = lambda a: a.reshape(crops, length, heads, HEAD)
    q4, k4, v4 = (split(q), split(k), split(v))
    ein = partial(jnp.einsum, preferred_element_type=f32)
    probs = jax.nn.softmax(ein("cqhd,ckhd->chqk", q4, k4) * scaling, axis=-1)
    low = probs.astype(bf16)
    mixed = ein("chqk,ckhd->cqhd", low, v4).astype(bf16).reshape(crops * length, width)
    hidden = rows + (dot(mixed, wo, ((1,), (0,))) + b_out)
    normed2, scaled2, inverse2 = normalize(hidden, mid_gain, mid_shift)
    normed2 = normed2.astype(bf16)
    upward = dot(normed2, wu, ((1,), (1,))) + bias[2]
    act32, gelu_pull = jax.vjp(partial(jax.nn.gelu, approximate=True), upward)
    act = act32.astype(bf16)
    result = hidden + (dot(act, wd, ((1,), (0,))) + b_down)
    latents_out = (result * live).astype(bf16).reshape(latents.shape)
    gy = cotangent.reshape(crops * length, width) * live.astype(bf16)
    g_wd = dot(act, gy, ((0,), (0,)))
    gu = gelu_pull(dot(gy, wd, ((1,), (1,))))[0].astype(bf16)
    g_wu = dot(gu, normed2, ((0,), (0,)))
    gn2 = dot(gu, wu, ((1,), (0,)))
    gh = gy.astype(f32) + norm_backward(gn2, scaled2, inverse2, mid_gain)
    ga = gh.astype(bf16)
    g_wo = dot(mixed, ga, ((0,), (0,)))
    go = split(dot(ga, wo, ((1,), (1,))).astype(bf16))
    gp = ein("cqhd,ckhd->chqk", go, v4)
    gs = (probs * (gp - jnp.sum(probs * gp, axis=-1, keepdims=True))).astype(bf16)
    flat = lambda a: a.astype(bf16).reshape(crops * length, width)
    gq = flat(ein("chqk,ckhd->cqhd", gs, k4) * scaling)
    gk = flat(ein("chqk,cqhd->ckhd", gs, q4) * scaling)
    gv = flat(ein("chqk,cqhd->ckhd", low, go))
    g_wq, g_wk, g_wv = [dot(a, normed, ((0,), (0,))) for a in (gq, gk, gv)]
    gn1 = dot(gq, wq, ((1,), (0,))) + dot(gk, wk, ((1,), (0,))) + dot(gv, wv, ((1,), (0,)))
    latents_grad = (gh + norm_backward(gn1, scaled, inverse, pre_gain)).reshape(latents.shape)

    def total(parts):
        stacked = jnp.stack([p.astype(bf16).reshape(tensor, per, width) for p in parts], axis=1)
        part = lax.psum_scatter(stacked, "tensor", scatter_dimension=0, tiled=True)
        return lax.psum(part, "dp")[0].astype(f32)

    s_wd, s_wu, s_wo = total((g_wd, g_wu, g_wo))
    s_wq, s_wk, s_wv = total((g_wq, g_wk, g_wv))
    col = lambda a: jnp.sum(a, axis=0, dtype=f32)
    sums = lax.psum(
        jnp.stack(
            [
                col(gn1 * scaled),
                col(gn1),
                col(ga),
                col(gn2 * scaled2),
                col(gn2),
                col(gy),
                col(gq),
                col(gv),
                col(gu),
            ]
        ),
        ("dp", "tensor"),
    )
    mine = lax.dynamic_slice_in_dim(sums[6:], lax.axis_index("tensor") * per, per, axis=1)
    return (
        latents_out,
        latents_grad,
        sums[0],
        sums[1],
        s_wq.T,
        mine[0],
        s_wk.T,
        s_wv.T,
        mine[1],
        s_wo,
        sums[2],
        sums[3],
        sums[4],
        s_wu.T,
        mine[2],
        s_wd,
        sums[5],
    )


def solution(mesh):
    return jax.shard_map(
        shards,
        mesh=mesh,
        in_specs=(
            P(("dp", "tensor"), None, None),
            P(("dp", "tensor"), None, None),
            P(),
            P(),
            P(),
            P(),
            P(None, "tensor"),
            P("tensor"),
            P(None, "tensor"),
            P(None, "tensor"),
            P("tensor"),
            P("tensor", None),
            P(),
            P(),
            P(),
            P(None, "tensor"),
            P("tensor"),
            P("tensor", None),
            P(),
        ),
        out_specs=(
            P(("dp", "tensor"), None, None),
            P(("dp", "tensor"), None, None),
            P(),
            P(),
            P(None, "tensor"),
            P("tensor"),
            P(None, "tensor"),
            P(None, "tensor"),
            P("tensor"),
            P("tensor", None),
            P(),
            P(),
            P(),
            P(None, "tensor"),
            P("tensor"),
            P("tensor", None),
            P(),
        ),
        check_vma=False,
    )
```

profile of v0, /device:TPU:0, one launch (start us, length us, event | category | flops | bytes accessed | tf_op | source)
XLA Modules:
  0.0 419.4 jit_solution(4079117353360037108)
XLA Ops:
  7.3 1.3 copy.36
  8.6 1.2 copy.37
  16.9 6.3 %all_gather.11 = f32[3,1024]{1,0:T(4,128)S(1)} all-gather(f32[3,256]{1,0:T(4,128)S(1)} %pad_maximum_fusion.2), channel_id=1, replica_groups=mesh['dp'=8,'tensor'=4] {'tensor'}, dimensions={1}, use_global_device_ids=true | all-gather | bytes 15360 | tf_op jit(solution)/shard_map/all_gather | solution.py:64
  23.8 76.6 %all-gather.3.cloned.1.call-done = bf16[6144,1024]{1,0:T(8,128)(2,1)} async-done(((bf16[1536,1024]{1,0:T(8,128)(2,1)}), bf16[6144,1024]{1,0:T(8,128)(2,1)}) %all-gather.3.cloned.1.call-update) | async-done | bytes 12582928 | tf_op jit(solution)/shard_map/all_gather | solution.py:62
  100.4 9.0 %fusion.70 = (bf16[4,1,256,1024]{3,2,1,0:T(8,128)(2,1)}, bf16[4,1,256,1024]{3,2,1,0:T(8,128)(2,1)}, bf16[4,1,256,1024]{3,2,1,0:T(8,128)(2,1)}, bf16[4,1,256,1024...) fusion(bf16[4,6,256,1024]{3,2,1,0:T(8,128)(2,1)} %bitcast.191), kind=kLoop, calls=%fused_computation.118 | loop fusion | bytes 25165824 | tf_op jit(solution)/shard_map/slice | solution.py:63
  109.4 2.3 add_convert_fusion.1
  111.7 2.3 copy.63
  114.0 2.9 convolution_convert_fusion.7
  117.5 4.3 %fusion.40 = bf16[64,8,8,128]{3,2,1,0:T(8,128)(2,1)} fusion(bf16[1024,1024]{1,0:T(8,128)(2,1)} %bitcast.208, f32[1024]{0:T(1024)S(1)} %bitcast.240, bf16[1,512,1024]{2,1,0:T(8,128)(2,1)S(1)} %copy-done.1, f32[1024]{0:T(1024)S(1)} %copy-done.31, f32[1024]{0:T(1024)S(1)} %copy-done.24, f32[512]{0:T(512)S(1)} %add_rsqrt_fusion.1, ...), kind=kOutput, calls=%fused_computation.74 | convolution fusion | flops 1077936128 | bytes 4210688 | tf_op jit(solution)/shard_map/dot_general | solution.py:58
  121.8 5.5 %fusion.74 = (f32[8,512]{1,0:T(8,128)S(1)}, f32[8,512,512]{1,2,0:T(8,128)}) fusion(bf16[512,8,128]{0,2,1:T(8,128)(2,1)S(1)} %bitcast.203, bf16[512,8,128]{0,2,1:T(8,128)(2,1)S(1)} %bitcast.204), kind=kOutput, calls=%fused_computation.122 | convolution fusion | flops 543162880 | bytes 10502144 | tf_op jit(solution)/shard_map/sub | solution.py:74
  127.3 4.7 %fusion.34 = bf16[8,128,512]{2,1,0:T(8,128)(2,1)S(1)} fusion(bf16[64,8,8,128]{3,2,1,0:T(8,128)(2,1)} %fusion.40, f32[8,512,512]{1,2,0:T(8,128)} %get-tuple-element.72, f32[8,512]{1,0:T(8,128)S(1)} %get-tuple-element.71), kind=kOutput, calls=%fused_computation.70 | convolution fusion | flops 541589504 | bytes 10502144 | tf_op jit(solution)/shard_map/chqk,ckhd->cqhd/dot_general | solution.py:76
  132.0 1.4 fusion.75
  133.8 1.2 copy-done.15
  135.0 1.3 fusion.63
  136.4 1.7 convolution_convert_fusion.2
  138.7 2.5 convert_reduce_fusion.2
  141.2 1.8 multiply_reduce_fusion.2
  143.0 1.5 convolution_convert_fusion.1
  144.5 0.9 convert_reduce_fusion.5
  145.5 1.3 convolution_convert_fusion
  146.8 3.4 pad_maximum_fusion.1
  150.2 4.5 %convolution_convert_fusion.6 = bf16[512,1024]{1,0:T(8,128)(2,1)} fusion(bf16[1024,1024]{1,0:T(8,128)(2,1)} %bitcast.196, f32[512,1024]{1,0:T(8,128)} %copy-done.5), kind=kOutput, calls=%fused_computation.72 | convolution fusion | flops 1074790400 | bytes 5242880 | tf_op jit(solution)/shard_map/dot_general | solution.py:58
  154.7 2.5 copy.65
  157.2 7.1 %convert_reduce_fusion.3 = (f32[8,128]{1,0:T(8,128)S(1)}, bf16[8,128,512]{2,1,0:T(8,128)(2,1)S(1)}) fusion(bf16[512,8,128]{0,2,1:T(8,128)(2,1)} %bitcast.218, f32[8,512,512]{1,2,0:T(8,128)} %get-tuple-element.72, f32[8,512]{1,0:T(8,128)S(1)} %get-tuple-element.71), kind=kOutput, calls=%fused_computation.43 | convolution fusion | flops 542637056 | bytes 10506240 | tf_op jit(solution)/shard_map/chqk,cqhd->ckhd/dot_general | solution.py:99
  164.3 2.7 convolution_convert_fusion.3
  167.0 3.9 copy.54
  170.9 6.2 %multiply_reduce_fusion = (f32[8,512]{1,0:T(8,128)S(1)}, f32[8,512,512]{1,2,0:T(8,128)S(1)}) fusion(f32[8,512,512]{1,2,0:T(8,128)} %get-tuple-element.72, f32[8,512]{1,0:T(8,128)S(1)} %get-tuple-element.71, bf16[512,8,128]{0,2,1:T(8,128)(2,1)} %bitcast.219, bf16[64,8,8,128]{3,2,1,0:T(8,128)(2,1)} %fusion.40), kind=kOutput, calls=%fused_computation.2 | convolution fusion | flops 543158272 | bytes 18907136 | tf_op jit(solution)/shard_map/cqhd,ckhd->chqk/dot_general | solution.py:94
  177.1 4.5 %multiply_convert_fusion = bf16[8,512,512]{1,2,0:T(8,128)(2,1)S(1)} fusion(f32[8,512,512]{1,2,0:T(8,128)S(1)} %get-tuple-element.77, f32[8,512]{1,0:T(8,128)S(1)} %get-tuple-element.76, f32[8,512,512]{1,2,0:T(8,128)} %get-tuple-element.72, f32[8,512]{1,0:T(8,128)S(1)} %get-tuple-element.71), kind=kLoop, calls=%fused_computation.1 | loop fusion | flops 8388608 | bytes 21004288 | tf_op jit(solution)/shard_map/convert_element_type | solution.py:95
  182.5 1.1 copy-done
  183.6 2.7 convolution_convert_fusion.5
  186.3 4.0 copy.52
  190.3 4.0 multiply_convert_fusion.1
  194.3 2.8 convolution_convert_fusion.4
  197.1 4.0 copy.53
  201.0 6.5 %pad_maximum_fusion = bf16[4,3,256,1024]{2,3,1,0:T(8,128)(2,1)} fusion(bf16[4,1,256,1024]{2,3,1,0:T(8,128)(2,1)} %copy.54, bf16[4,1,256,1024]{2,3,1,0:T(8,128)(2,1)} %copy.53, bf16[4,1,256,1024]{2,3,1,0:T(8,128)(2,1)} %copy.52), kind=kLoop, calls=%fused_computation.6 | loop fusion | flops 6291456 | bytes 12582912 | tf_op jit(solution)/shard_map/stack | solution.py:105
  207.8 1.4 reduce-scatter.5.cloned.1.call-done
  209.2 61.4 %reduce-scatter.3.cloned.1.call-done = bf16[1,3,256,1024]{2,3,1,0:T(8,128)(2,1)} async-done(((bf16[4,3,256,1024]{2,3,1,0:T(8,128)(2,1)}), bf16[1,3,256,1024]{2,3,1,0:T(8,128)(2,1)}) %reduce-scatter.3.cloned.1.call-update) | async-done | bytes 1572880 | tf_op jit(solution)/shard_map/reduce_scatter | solution.py:106
  270.6 3.3 fusion.77
  274.0 1.3 fusion.76
  275.8 3.3 fusion.17
  279.2 42.9 %psum.21 = f32[9,1024]{1,0:T(8,128)S(1)} all-reduce(f32[9,1024]{1,0:T(8,128)S(1)} %stack.61), channel_id=1, replica_groups=mesh['dp'=8,'tensor'=4] {'dp','tensor'}, use_global_device_ids=true, to_apply=%region_21.22 | all-reduce | flops 9216 | bytes 73728 | tf_op jit(solution)/shard_map/psum | solution.py:112
  323.5 4.4 %fusion.16 = f32[1,512,1024]{2,1,0:T(8,128)} fusion(f32[512,1024]{1,0:T(8,128)} %copy-done.5, bf16[1,512,1024]{2,1,0:T(8,128)(2,1)S(1)} %copy-done.1, f32[512,1024]{1,0:T(8,128)} %get-tuple-element.78, f32[512]{0:T(512)S(1)} %broadcast_multiply_fusion, f32[512]{0:T(512)S(1)} %broadcast_multiply_fusion.1, f32[1024]{0:T(1024)S(1)} %copy-done.24, ...), kind=kLoop, calls=%fused_computation.28 | loop fusion | flops 4718592 | bytes 7352320 | tf_op jit(solution)/shard_map/reshape | solution.py:102
  327.9 2.6 fusion.41
  330.5 73.5 %all-reduce.3.cloned.1.call-done = (bf16[1,3,256,1024]{2,3,1,0:T(8,128)(2,1)}, bf16[1,3,256,1024]{3,2,1,0:T(8,128)(2,1)}) async-done(((bf16[1,3,256,1024]{2,3,1,0:T(8,128)(2,1)}, bf16[1,3,256,1024]{3,2,1,0:T(8,128)(2,1)}), (bf16[1,3,256,1024]{2,3,1,0:T(8,128)(2,1)}, bf16[1,3,256,1024]{3,2,1,0:T(8,128)(2,1)})) %all-reduce.3.cloned.1.call-update) | async-done | bytes 3145744 | tf_op jit(solution)/shard_map/psum | solution.py:107
  403.9 1.7 convert_element_type.173
  405.6 1.7 slice_bitcast_fusion.3
  408.4 1.8 slice_bitcast_fusion
  410.2 2.5 copy.58
  (108 shorter events, 12.7 us)
Async XLA Ops:
  7.2 2.7 copy-start.18
  7.2 2.9 copy-start.19
  7.2 93.2 %all-gather.3.cloned.1.call-start = ((), (), s32[]{:S(2)}) async-start(), calls=%async_computation.4 | async-start | bytes 15728640 | tf_op jit(solution)/shard_map/all_gather | solution.py:62
  10.1 2.8 copy-start.20
  11.2 3.4 copy-start.21
  14.5 1.0 copy-start.28
  14.5 1.0 copy-start.29
  14.5 2.3 copy-start.25
  14.5 2.3 copy-start.26
  14.6 2.3 copy-start.27
  14.6 8.6 %copy-start.1 = (bf16[1,512,1024]{2,1,0:T(8,128)(2,1)S(1)}, bf16[1,512,1024]{2,1,0:T(8,128)(2,1)}, u32[]{:S(2)}) copy-start(bf16[1,512,1024]{2,1,0:T(8,128)(2,1)} %param.19) | copy-start | bytes 3145732
  15.5 193.7 %reduce-scatter.5.cloned.1.call-start = ((), (), s32[]{:S(2)}) async-start(), calls=%async_computation.3 | async-start | bytes 7864320 | tf_op jit(solution)/shard_map/reduce_scatter | solution.py:106
  100.4 9.0 %copy-start.24 = (f32[1024]{0:T(1024)S(1)}, f32[1024]{0:T(1024)}, u32[]{:S(2)}) copy-start(f32[1024]{0:T(1024)} %param.23) | copy-start | bytes 12292
  100.4 9.0 %copy-start.31 = (f32[1024]{0:T(1024)S(1)}, f32[1024]{0:T(1024)}, u32[]{:S(2)}) copy-start(f32[1024]{0:T(1024)} %param.24) | copy-start | bytes 12292
  109.4 2.3 copy-start.2
  117.5 4.3 %copy-start.10 = (bf16[512,1024]{0,1:T(8,128)(2,1)}, bf16[512,1024]{0,1:T(8,128)(2,1)S(1)}, u32[]{:S(2)}) copy-start(bf16[512,1024]{0,1:T(8,128)(2,1)S(1)} %copy.64) | copy-start | bytes 3145732
  117.5 4.3 %copy-start.9 = (bf16[512,1024]{0,1:T(8,128)(2,1)S(1)}, bf16[512,1024]{0,1:T(8,128)(2,1)}, u32[]{:S(2)}) copy-start(bf16[512,1024]{0,1:T(8,128)(2,1)} %copy.63) | copy-start | bytes 3145732
  127.3 4.8 %copy-start.4 = (bf16[4,1,256,1024]{3,2,1,0:T(8,128)(2,1)S(1)}, bf16[4,1,256,1024]{3,2,1,0:T(8,128)(2,1)}, u32[]{:S(2)}) copy-start(bf16[4,1,256,1024]{3,2,1,0:T(8,128)(2,1)} %get-tuple-element.48) | copy-start | bytes 6291460
  127.3 4.8 %copy-start.22 = (f32[1024]{0:T(1024)S(1)}, f32[1024]{0:T(1024)}, u32[]{:S(2)}) copy-start(f32[1024]{0:T(1024)} %param.31) | copy-start | bytes 12292
  133.4 1.6 copy-start.15
  133.4 1.6 copy-start.23
  133.4 1.6 copy-start.30
  135.0 1.4 copy-start.17
  136.4 1.7 copy-start.35
  136.4 2.3 copy-start.12
  145.5 1.3 copy-start.5
  150.2 120.4 %reduce-scatter.3.cloned.1.call-start = ((), (), s32[]{:S(2)}) async-start(), calls=%async_computation.2 | async-start | bytes 7864320 | tf_op jit(solution)/shard_map/reduce_scatter | solution.py:106
  164.3 2.7 copy-start.33
  177.1 4.5 %copy-start.11 = (bf16[512,1024]{0,1:T(8,128)(2,1)S(1)}, bf16[512,1024]{0,1:T(8,128)(2,1)}, u32[]{:S(2)}) copy-start(bf16[512,1024]{0,1:T(8,128)(2,1)} %copy-done.10) | copy-start | bytes 3145732
  181.6 1.9 copy-start
  183.6 2.7 copy-start.6
  194.3 2.8 copy-start.8
  207.5 196.4 %all-reduce.3.cloned.1.call-start = ((), (), s32[]{:S(2)}) async-start(), calls=%async_computation.5 | async-start | bytes 6291456 | tf_op jit(solution)/shard_map/psum | solution.py:107
  270.6 3.4 copy-start.3
  270.6 3.4 copy-start.7
  274.0 1.6 copy-start.14
  274.0 1.8 copy-start.34
  323.5 4.4 %copy-start.13 = (bf16[4,1,256,1024]{3,2,1,0:T(8,128)(2,1)S(1)}, bf16[4,1,256,1024]{3,2,1,0:T(8,128)(2,1)}, u32[]{:S(2)}) copy-start(bf16[4,1,256,1024]{3,2,1,0:T(8,128)(2,1)} %get-tuple-element.47) | copy-start | bytes 6291460
  323.5 4.4 %copy-start.32 = (f32[1024]{0:T(1024)S(1)}, f32[1024]{0:T(1024)}, u32[]{:S(2)}) copy-start(f32[1024]{0:T(1024)} %param.37) | copy-start | bytes 12292
  323.5 4.4 %copy-start.36 = (f32[512,1024]{1,0:T(8,128)S(1)}, f32[512,1024]{1,0:T(8,128)}, u32[]{:S(2)}) copy-start(f32[512,1024]{1,0:T(8,128)} %copy-done.35) | copy-start | bytes 6291460
  405.6 2.4 copy-start.16
Sparse Core Ops, SparseCore 0:
  15.6 84.7 all-gather.2
  150.3 58.8 reduce-scatter.4
  211.7 58.8 reduce-scatter.2
  274.1 129.8 all-reduce.2
where the time goes:
time: 426 us; the launch traced here: 419 us
  waiting for transfers between devices  213 us (50%)
  matrix products  72.4 us (17%)
  blocking collectives  49.2 us (12%)
  local copies, waits for them, and re-layouts  45.9 us (11%)
  other arithmetic  23.3 us (5%)
  between operations  15.2 us (4%)
    all_gather x1, waiting for transfers between devices, shards(): lax.all_gather(columns, 'tensor', axis=0, tiled=False)  76.6 us
    psum x1, waiting for transfers between devices, total(): return lax.psum(part, 'dp')[0].astype(f32)  73.5 us
    reduce_scatter x2, waiting for transfers between devices, total(): part = lax.psum_scatter(stacked, 'tensor', scatter_dimension=0, tiled=True)  62.8 us
    dot_general x18, matrix products, dot(): lax.dot_general(left, right, (dims, ((), ())), preferred_element_type=f32)  44 us
    psum x1, blocking collectives, shards(): lax.psum(jnp.stack([col(gn1 * scaled), col(gn1), col(ga), col(gn2 * scale...  42.9 us
    unnamed x84, local copies, waits for them, and re-layouts  14.1 us
    another operation x3, local copies, waits for them, and re-layouts, total(): jnp.stack([p.astype(bf16).reshape(tensor, per, width) for p in parts], ax...  11.8 us
    another operation x2, other arithmetic, total(): jnp.stack([p.astype(bf16).reshape(tensor, per, width) for p in parts], ax...  9.82 us
  transfers between devices with their start and end apart: 4, of which 4 were waited for; matrix products, arithmetic and copies ran while one was open for 18% of the time, Pallas kernels for 0%

commit v1 on v0

--- a/solution.py
+++ b/solution.py
@@ -109,21 +109,24 @@
     s_wd, s_wu, s_wo = total((g_wd, g_wu, g_wo))
     s_wq, s_wk, s_wv = total((g_wq, g_wk, g_wv))
     col = lambda a: jnp.sum(a, axis=0, dtype=f32)
-    sums = lax.psum(
-        jnp.stack(
-            [
-                col(gn1 * scaled),
-                col(gn1),
-                col(ga),
-                col(gn2 * scaled2),
-                col(gn2),
-                col(gy),
-                col(gq),
-                col(gv),
-                col(gu),
-            ]
+    sums = jnp.sum(
+        lax.all_gather(
+            jnp.stack(
+                [
+                    col(gn1 * scaled),
+                    col(gn1),
+                    col(ga),
+                    col(gn2 * scaled2),
+                    col(gn2),
+                    col(gy),
+                    col(gq),
+                    col(gv),
+                    col(gu),
+                ]
+            ),
+            ("dp", "tensor"),
         ),
-        ("dp", "tensor"),
+        axis=0,
     )
     mine = lax.dynamic_slice_in_dim(sums[6:], lax.axis_index("tensor") * per, per, axis=1)
     return (

time: 426 us -> 484 us (1.14)
  waiting for transfers between devices: 213 us -> 310 us
  blocking collectives: 49.2 us -> 6.27 us
    psum x1, waiting for transfers between devices: 73.5 us -> 128 us  [total(): return lax.psum(part, 'dp')[0].astype(f32)]
    all_gather x0 -> x1, waiting for transfers between devices: none -> 52.5 us  [shards(): lax.all_gather(jnp.stack([col(gn1 * scaled), col(gn1), col(ga), col(gn2 *...]
    psum x1 -> x0, blocking collectives: 42.9 us -> none  [shards(): lax.psum(jnp.stack([col(gn1 * scaled), col(gn1), col(ga), col(gn2 * scale...]
    reduce_scatter x2, waiting for transfers between devices: 62.8 us -> 52.9 us  [total(): part = lax.psum_scatter(stacked, 'tensor', scatter_dimension=0, tiled=True)]
  transfers between devices with their start and end apart: 4 -> 5, of which waited for: 4 -> 4; matrix products, arithmetic and copies ran while one was open for 18% -> 16% of each run, Pallas kernels for 0% -> 0%
where the time goes in v1:
time: 484 us; the launch traced here: 477 us
  waiting for transfers between devices  310 us (64%)
  matrix products  72.4 us (15%)
  local copies, waits for them, and re-layouts  47.1 us (10%)
  other arithmetic  25.1 us (5%)
  between operations  15.3 us (3%)
  blocking collectives  6.27 us (1%)
    psum x1, waiting for transfers between devices, total(): return lax.psum(part, 'dp')[0].astype(f32)  128 us
    all_gather x1, waiting for transfers between devices, shards(): lax.all_gather(columns, 'tensor', axis=0, tiled=False)  76.6 us
    reduce_scatter x2, waiting for transfers between devices, total(): part = lax.psum_scatter(stacked, 'tensor', scatter_dimension=0, tiled=True)  52.9 us
    all_gather x1, waiting for transfers between devices, shards(): lax.all_gather(jnp.stack([col(gn1 * scaled), col(gn1), col(ga), col(gn2 *...  52.5 us
    dot_general x18, matrix products, dot(): lax.dot_general(left, right, (dims, ((), ())), preferred_element_type=f32)  44.1 us
    unnamed x84, local copies, waits for them, and re-layouts  14.1 us
    another operation x3, local copies, waits for them, and re-layouts, total(): jnp.stack([p.astype(bf16).reshape(tensor, per, width) for p in parts], ax...  11.8 us
    another operation x2, other arithmetic, total(): jnp.stack([p.astype(bf16).reshape(tensor, per, width) for p in parts], ax...  9.82 us
  transfers between devices with their start and end apart: 5, of which 4 were waited for; matrix products, arithmetic and copies ran while one was open for 16% of the time, Pallas kernels for 0%

profile of v1, /device:TPU:0, one launch (start us, length us, event | category | flops | bytes accessed | tf_op | source)
XLA Modules:
  0.0 477.0 jit_solution(2687523989882324035)
XLA Ops:
  7.3 1.3 copy.59
  8.6 1.2 copy.60
  16.9 6.3 %all_gather.17 = f32[3,1024]{1,0:T(4,128)S(1)} all-gather(f32[3,256]{1,0:T(4,128)S(1)} %pad_maximum_fusion.2), channel_id=1, replica_groups=mesh['dp'=8,'tensor'=4] {'tensor'}, dimensions={1}, use_global_device_ids=true | all-gather | bytes 15360 | tf_op jit(solution)/shard_map/all_gather | solution.py:64
  23.8 76.6 %all-gather.6.cloned.1.call-done = bf16[6144,1024]{1,0:T(8,128)(2,1)} async-done(((bf16[1536,1024]{1,0:T(8,128)(2,1)}), bf16[6144,1024]{1,0:T(8,128)(2,1)}) %all-gather.6.cloned.1.call-update) | async-done | bytes 12582928 | tf_op jit(solution)/shard_map/all_gather | solution.py:62
  100.4 8.9 %fusion.70 = (bf16[4,1,256,1024]{3,2,1,0:T(8,128)(2,1)}, bf16[4,1,256,1024]{3,2,1,0:T(8,128)(2,1)}, bf16[4,1,256,1024]{3,2,1,0:T(8,128)(2,1)}, bf16[4,1,256,1024...) fusion(bf16[4,6,256,1024]{3,2,1,0:T(8,128)(2,1)} %bitcast.192), kind=kLoop, calls=%fused_computation.118 | loop fusion | bytes 25165824 | tf_op jit(solution)/shard_map/slice | solution.py:63
  109.4 2.3 add_convert_fusion.1
  111.7 2.3 copy.86
  113.9 2.9 convolution_convert_fusion.7
  117.4 4.3 fusion.40
  121.7 5.5 %fusion.74 = (f32[8,512]{1,0:T(8,128)S(1)}, f32[8,512,512]{1,2,0:T(8,128)}) fusion(bf16[512,8,128]{0,2,1:T(8,128)(2,1)S(1)} %bitcast.204, bf16[512,8,128]{0,2,1:T(8,128)(2,1)S(1)} %bitcast.205), kind=kOutput, calls=%fused_computation.122 | convolution fusion | flops 543162880 | bytes 10502144 | tf_op jit(solution)/shard_map/sub | solution.py:74
  127.2 4.7 fusion.34
  132.0 1.4 fusion.75
  133.8 1.2 copy-done.15
  135.0 1.3 fusion.63
  136.3 1.7 convolution_convert_fusion.2
  138.7 2.5 convert_reduce_fusion.2
  141.2 1.8 multiply_reduce_fusion.2
  143.0 1.5 convolution_convert_fusion.1
  145.4 1.3 convolution_convert_fusion
  146.7 3.4 pad_maximum_fusion.1
  150.2 4.5 convolution_convert_fusion.6
  154.7 2.5 copy.88
  157.1 7.1 %convert_reduce_fusion.3 = (f32[8,128]{1,0:T(8,128)S(1)}, bf16[8,128,512]{2,1,0:T(8,128)(2,1)S(1)}) fusion(bf16[512,8,128]{0,2,1:T(8,128)(2,1)} %bitcast.219, f32[8,512,512]{1,2,0:T(8,128)} %get-tuple-element.89, f32[8,512]{1,0:T(8,128)S(1)} %get-tuple-element.88), kind=kOutput, calls=%fused_computation.43 | convolution fusion | flops 542637056 | bytes 10506240 | tf_op jit(solution)/shard_map/chqk,cqhd->ckhd/dot_general | solution.py:99
  164.2 2.7 convolution_convert_fusion.3
  166.9 3.9 copy.77
  170.9 6.2 %multiply_reduce_fusion = (f32[8,512]{1,0:T(8,128)S(1)}, f32[8,512,512]{1,2,0:T(8,128)S(1)}) fusion(f32[8,512,512]{1,2,0:T(8,128)} %get-tuple-element.89, f32[8,512]{1,0:T(8,128)S(1)} %get-tuple-element.88, bf16[512,8,128]{0,2,1:T(8,128)(2,1)} %bitcast.220, bf16[64,8,8,128]{3,2,1,0:T(8,128)(2,1)} %fusion.40), kind=kOutput, calls=%fused_computation.2 | convolution fusion | flops 543158272 | bytes 18907136 | tf_op jit(solution)/shard_map/cqhd,ckhd->chqk/dot_general | solution.py:94
  177.1 4.5 multiply_convert_fusion
  182.4 1.1 copy-done
  183.5 2.7 convolution_convert_fusion.5
  186.3 4.0 copy.75
  190.2 4.0 multiply_convert_fusion.1
  194.3 2.8 convolution_convert_fusion.4
  197.0 4.0 copy.76
  201.0 6.5 %pad_maximum_fusion = bf16[4,3,256,1024]{2,3,1,0:T(8,128)(2,1)} fusion(bf16[4,1,256,1024]{2,3,1,0:T(8,128)(2,1)} %copy.77, bf16[4,1,256,1024]{2,3,1,0:T(8,128)(2,1)} %copy.76, bf16[4,1,256,1024]{2,3,1,0:T(8,128)(2,1)} %copy.75), kind=kLoop, calls=%fused_computation.6 | loop fusion | flops 6291456 | bytes 12582912 | tf_op jit(solution)/shard_map/stack | solution.py:105
  207.8 3.5 fusion.77
  211.3 1.3 fusion.76
  213.1 3.2 fusion.17
  216.4 1.3 stack.61
  217.7 52.8 %reduce-scatter.3.cloned.1.call-done = bf16[1,3,256,1024]{2,3,1,0:T(8,128)(2,1)} async-done(((bf16[4,3,256,1024]{2,3,1,0:T(8,128)(2,1)}), bf16[1,3,256,1024]{2,3,1,0:T(8,128)(2,1)}) %reduce-scatter.3.cloned.1.call-update) | async-done | bytes 1572880 | tf_op jit(solution)/shard_map/reduce_scatter | solution.py:106
  270.7 4.4 fusion.16
  275.1 2.6 fusion.41
  277.6 52.5 %all-gather.8.cloned.1.call-done = f32[32,9,1024]{2,1,0:T(8,128)} async-done(((f32[1,9,1024]{2,1,0:T(8,128)}), f32[32,9,1024]{2,1,0:T(8,128)}) %all-gather.8.cloned.1.call-update) | async-done | bytes 1179664 | tf_op jit(solution)/shard_map/all_gather | solution.py:113
  330.2 1.7 reduce_sum.209
  333.2 128.3 %all-reduce.3.cloned.1.call-done = (bf16[1,3,256,1024]{2,3,1,0:T(8,128)(2,1)}, bf16[1,3,256,1024]{3,2,1,0:T(8,128)(2,1)}) async-done(((bf16[1,3,256,1024]{2,3,1,0:T(8,128)(2,1)}, bf16[1,3,256,1024]{3,2,1,0:T(8,128)(2,1)}), (bf16[1,3,256,1024]{2,3,1,0:T(8,128)(2,1)}, bf16[1,3,256,1024]{3,2,1,0:T(8,128)(2,1)})) %all-reduce.3.cloned.1.call-update) | async-done | bytes 3145744 | tf_op jit(solution)/shard_map/psum | solution.py:107
  461.5 1.7 convert_element_type.173
  463.2 1.7 slice_bitcast_fusion.3
  465.9 1.8 slice_bitcast_fusion
  467.7 2.5 copy.81
  (111 shorter events, 13.7 us)
Async XLA Ops:
  7.2 2.7 copy-start.18
  7.2 2.9 copy-start.19
  7.2 93.2 %all-gather.6.cloned.1.call-start = ((), (), s32[]{:S(2)}) async-start(), calls=%async_computation.4 | async-start | bytes 15728640 | tf_op jit(solution)/shard_map/all_gather | solution.py:62
  10.1 2.8 copy-start.20
  11.2 3.4 copy-start.21
  14.5 1.0 copy-start.28
  14.5 1.0 copy-start.29
  14.5 2.3 copy-start.25
  14.5 2.3 copy-start.26
  14.6 2.3 copy-start.27
  14.6 8.6 %copy-start.1 = (bf16[1,512,1024]{2,1,0:T(8,128)(2,1)S(1)}, bf16[1,512,1024]{2,1,0:T(8,128)(2,1)}, u32[]{:S(2)}) copy-start(bf16[1,512,1024]{2,1,0:T(8,128)(2,1)} %param.19) | copy-start | bytes 3145732
  15.5 202.3 %reduce-scatter.5.cloned.1.call-start = ((), (), s32[]{:S(2)}) async-start(), calls=%async_computation.3 | async-start | bytes 7864320 | tf_op jit(solution)/shard_map/reduce_scatter | solution.py:106
  100.4 8.9 %copy-start.24 = (f32[1024]{0:T(1024)S(1)}, f32[1024]{0:T(1024)}, u32[]{:S(2)}) copy-start(f32[1024]{0:T(1024)} %param.23) | copy-start | bytes 12292
  100.4 9.0 %copy-start.31 = (f32[1024]{0:T(1024)S(1)}, f32[1024]{0:T(1024)}, u32[]{:S(2)}) copy-start(f32[1024]{0:T(1024)} %param.24) | copy-start | bytes 12292
  109.4 2.3 copy-start.2
  117.4 4.3 copy-start.10
  117.4 4.3 copy-start.9
  127.2 4.8 copy-start.4
  127.2 4.8 copy-start.22
  133.4 1.6 copy-start.15
  133.4 1.6 copy-start.23
  133.4 1.6 copy-start.30
  135.0 1.4 copy-start.17
  136.3 1.7 copy-start.35
  136.3 2.3 copy-start.12
  145.4 1.3 copy-start.5
  150.1 120.5 %reduce-scatter.3.cloned.1.call-start = ((), (), s32[]{:S(2)}) async-start(), calls=%async_computation.2 | async-start | bytes 7864320 | tf_op jit(solution)/shard_map/reduce_scatter | solution.py:106
  164.2 2.7 copy-start.33
  177.1 4.5 copy-start.11
  181.6 1.9 copy-start
  183.5 2.7 copy-start.6
  194.3 2.8 copy-start.8
  207.5 122.7 %all-gather.8.cloned.1.call-start = ((), (), s32[]{:S(2)}) async-start(), calls=%async_computation.5 | async-start | bytes 2162688 | tf_op jit(solution)/shard_map/all_gather | solution.py:113
  207.7 3.5 copy-start.3
  207.8 3.5 copy-start.7
  211.3 1.6 copy-start.14
  211.3 1.8 copy-start.34
  217.7 243.8 %all-reduce.3.cloned.1.call-start = ((), (), s32[]{:S(2)}) async-start(), calls=%async_computation.6 | async-start | bytes 6291456 | tf_op jit(solution)/shard_map/psum | solution.py:107
  270.6 4.4 copy-start.13
  270.7 4.4 copy-start.32
  270.7 4.4 copy-start.36
  463.2 2.4 copy-start.16
Sparse Core Ops, SparseCore 0:
  15.6 84.7 all-gather.5
  150.2 58.8 reduce-scatter.4
  211.7 58.8 reduce-scatter.2
  273.9 56.2 all-gather.7
  333.7 127.7 all-reduce.2
